TPU v7x, 256 devices: a whole 4x4x8 slice. The times are simulated.
256 devices in a mesh: seq: 64 (over y, z, core), tp: 4 (over x).
Axes of the slice: x: 4, y: 4, z: 8, core: 2. Of those that a mesh axis runs over, the one named last changes fastest.
Arguments:
- tokens: bfloat16 [49152, 4096], P('seq'), may hold values from -6 to 6
- query_weight: bfloat16 [4096, 2048], P('seq', 'tp'), may hold values from -0.09375 to 0.09375
- key_weight: bfloat16 [4096, 2048], P('seq', 'tp'), may hold values from -0.09375 to 0.09375
- value_weight: bfloat16 [4096, 2048], P('seq', 'tp'), may hold values from -0.09375 to 0.09375
- gate_weight: bfloat16 [4096, 16], P('seq', 'tp'), may hold values from -0.09375 to 0.09375
- decay_rate: float32 [16], P('tp'), may hold values from 4.0690106e-06 to 0.04
- norm_gain: float32 [2048], P('tp'), may hold values from 0.5 to 1.5
- out_weight: bfloat16 [2048, 4096], P(None, 'tp'), may hold values from -0.125 to 0.125
Outputs:
- mixed: bfloat16 [49152, 4096], P('seq', 'tp')
All inputs are finite; a program needn't handle non-finite values.
Results may differ from a plain program's by a relative error of at most 0.006.
The roundings to bfloat16 on the way count: a program that leaves them out, or rounds other values in their place, can miss the bound.
Values may be sent and summed in bfloat16 or wider, within the bound.
A program may use at most 128 MiB of HBM per device.

v0:
```python
import jax
import jax.numpy as jnp
from jax import lax
from jax.sharding import Mesh
from jax.sharding import PartitionSpec as P

SEQ = ("seq_0", "seq_1", "seq_2")


def side_by_side(arrays, axis, dim, along):
    both = jnp.concatenate(arrays, axis=along)
    whole, at, finished = (lax.all_gather(both, axis, axis=dim, tiled=True), 0, [])
    for a in arrays:
        finished.append(lax.slice_in_dim(whole, at, at + a.shape[along], axis=along))
        at += a.shape[along]
    return tuple(finished)


def nothing_yet(shard, identity):
    return jax.tree.map(
        lambda part, zero: jnp.zeros_like(part) + jnp.asarray(zero, part.dtype), shard, identity
    )


def carried_in(shard, axes, combine, identity):
    before = start = nothing_yet(shard, identity)
    so_far = shard
    for axis in reversed(axes):
        peers, position = (lax.axis_size(axis), lax.axis_index(axis))
        pieces = jax.tree.map(lambda part: lax.all_gather(part, axis), so_far)
        inside, so_far = (start, start)
        for k in range(peers):
            passed = k < position
            so_far = combine(so_far, jax.tree.map(lambda part: part[k], pieces))
            inside = jax.tree.map(lambda new, old: jnp.where(passed, new, old), so_far, inside)
        before = combine(inside, before)
    return before


def on_device(
    tokens, query_weight, key_weight, value_weight, gate_weight, decay_rate, norm_gain, out_weight
):
    tok_rows = tokens.shape[0]
    head_count = decay_rate.shape[0]
    proj_width = query_weight.shape[1]
    head_size = proj_width // head_count

    def contract(piece):
        return jnp.dot(tokens, piece, preferred_element_type=jnp.float32)

    pieces = side_by_side((query_weight, key_weight, value_weight, gate_weight), SEQ, 0, 1)
    query_proj, key_proj, value_proj, gate_logit = tuple(
        (contract(one_piece) for one_piece in pieces)
    )
    query_heads = query_proj.astype(jnp.bfloat16).reshape(tok_rows, head_count, head_size)
    key_heads = key_proj.astype(jnp.bfloat16).reshape(tok_rows, head_count, head_size)
    value_per_head = value_proj.astype(jnp.bfloat16).reshape(tok_rows, head_count, head_size)
    log_decay = -decay_rate[None, :] * jax.nn.softplus(gate_logit)
    within = jnp.cumsum(log_decay, axis=0)
    block_total = within[-1]
    key_scaled = (jnp.exp(block_total[None, :] - within)[:, :, None] * key_heads).astype(
        jnp.bfloat16
    )
    shard_local_state = jnp.einsum(
        "gfw,gfz->fwz", key_scaled, value_per_head, preferred_element_type=jnp.float32
    )

    def decayed_join(earlier, later):
        return (earlier[0] + later[0], jnp.exp(later[0])[:, None, None] * earlier[1] + later[1])

    _, prefix_state = carried_in(
        (block_total, shard_local_state),
        SEQ,
        decayed_join,
        (jnp.zeros_like(block_total), jnp.zeros_like(shard_local_state)),
    )
    query_scaled = (jnp.exp(within)[:, :, None] * query_heads).astype(jnp.bfloat16)
    carried_state = jnp.einsum(
        "fys,ysu->fyu",
        query_scaled,
        prefix_state.astype(jnp.bfloat16),
        preferred_element_type=jnp.float32,
    )
    scores = jnp.einsum("thk,shk->hts", query_heads, key_heads, preferred_element_type=jnp.float32)
    row_index = lax.broadcasted_iota(jnp.int32, (tok_rows, tok_rows), 0)
    col_index = lax.broadcasted_iota(jnp.int32, (tok_rows, tok_rows), 1)
    causal = (col_index <= row_index)[None, :, :]
    decay_gap = within.T[:, :, None] - within.T[:, None, :]
    attn = jnp.where(causal, scores * jnp.exp(jnp.where(causal, decay_gap, 0.0)), 0.0).astype(
        jnp.bfloat16
    )
    local_part = jnp.einsum(
        "hts,shv->thv", attn, value_per_head, preferred_element_type=jnp.float32
    )
    head_out = carried_state + local_part
    mean_square = jnp.mean(head_out * head_out, axis=-1, keepdims=True)
    normed = (head_out * lax.rsqrt(mean_square + 1e-05)).reshape(tok_rows, proj_width) * norm_gain[
        None, :
    ]
    normed = normed.astype(jnp.bfloat16)
    mixed = jnp.dot(
        lax.all_gather(normed, "tp", axis=1, tiled=True),
        out_weight,
        preferred_element_type=jnp.float32,
    )
    return mixed.astype(jnp.bfloat16)


def solution(mesh):
    finer = Mesh(mesh.devices.reshape(4, 8, 2, mesh.shape["tp"]), ("seq_0", "seq_1", "seq_2", "tp"))
    return jax.shard_map(
        on_device,
        mesh=finer,
        in_specs=(
            P(SEQ, None),
            P(SEQ, "tp"),
            P(SEQ, "tp"),
            P(SEQ, "tp"),
            P(SEQ, "tp"),
            P("tp"),
            P("tp"),
            P(None, "tp"),
        ),
        out_specs=P(SEQ, "tp"),
        check_vma=False,
    )
```

profile of v0, /device:TPU:1, one launch (start us, length us, event | category | flops | bytes accessed | tf_op | source)
XLA Modules:
  0.0 258.8 jit_solution(4576178796495780604)
XLA Ops:
  6.5 0.0 all-gather.9.cloned.1.call-start
  6.5 0.8 copy.26
  7.3 1.6 pad_maximum_fusion
  8.9 0.0 all-gather.9.cloned.1.call-update
  8.9 0.0 all-gather.11.cloned.1.call-start
  9.0 0.7 neg.9
  9.7 96.5 %all-gather.9.cloned.1.call-done = bf16[4096,1540]{1,0:T(8,128)(2,1)} async-done(((bf16[64,1540]{1,0:T(8,128)(2,1)}), bf16[4096,1540]{1,0:T(8,128)(2,1)}) %all-gather.9.cloned.1.call-update) | async-done | bytes 12615696 | tf_op jit(solution)/shard_map/all_gather | solution.py:12
  106.2 0.0 slice-start
  106.2 5.0 %fusion.70 = f32[4,768]{1,0:T(4,128)S(1)} fusion(bf16[768,4096]{1,0:T(8,128)(2,1)} %param.8, bf16[4096,1540]{1,0:T(8,128)(2,1)} %all-gather.9.cloned.1.call-done, f32[4]{0:T(128)S(1)} %neg.9), kind=kOutput, calls=%fused_computation.90 | convolution fusion | flops 25187328 | bytes 7352336 | tf_op jit(solution)/shard_map/dot_general | solution.py:49
  111.2 1.1 reduce-window.6
  112.4 0.2 slice_reduce_fusion
  112.5 0.2 reduce-window.9
  112.7 0.1 add_bitcast_fusion
  112.8 0.2 slice_reduce_fusion.1
  113.0 0.1 subtract_exponential_fusion
  113.1 0.0 slice-start.1
  113.1 7.7 %fusion.15 = bf16[512,768]{1,0:T(8,128)(2,1)S(1)} fusion(bf16[768,4096]{1,0:T(8,128)(2,1)} %param.8, bf16[4096,1540]{1,0:T(8,128)(2,1)} %all-gather.9.cloned.1.call-done), kind=kOutput, calls=%fused_computation.21 | convolution fusion | flops 3221618688 | bytes 11272192 | tf_op jit(solution)/shard_map/dot_general | solution.py:49
  120.8 0.0 slice-done
  120.8 0.0 slice-done.1
  120.8 0.0 copy-start.1
  120.8 5.9 %fusion.12 = bf16[512,768]{1,0:T(8,128)(2,1)S(1)} fusion(bf16[768,4096]{1,0:T(8,128)(2,1)S(1)} %bitcast.238, bf16[4096,1540]{1,0:T(8,128)(2,1)} %all-gather.9.cloned.1.call-done), kind=kOutput, calls=%fused_computation.20 | convolution fusion | flops 3221618688 | bytes 11272192 | tf_op jit(solution)/shard_map/dot_general | solution.py:49
  126.7 0.0 copy-start.2
  126.7 0.0 copy-done.1
  126.8 0.4 fusion.23
  127.1 2.2 all-gather
  129.3 1.8 all-gather.1
  131.1 0.0 copy-done.2
  131.1 0.8 bitcast_add_fusion.8
  131.9 0.0 all-gather.11.cloned.1.call-update
  131.9 0.0 all-gather.13.cloned.1.call-start
  132.0 0.2 iota_compare_fusion
  132.2 11.1 %all-gather.2 = f32[8,1,4]{2,1,0:T(1,128)S(1)} all-gather(f32[1,1,4]{2,1,0:T(1,128)S(1)} %get-tuple-element.23), channel_id=1, replica_groups=mesh['seq_0'=4,'seq_1'=8,'seq_2'=2,'tp'=4] {'seq_1'}, dimensions={0}, use_global_device_ids=true | all-gather | bytes 144 | tf_op jit(solution)/shard_map/all_gather | solution.py:30
  143.4 22.0 %all-gather.11.cloned.1.call-done = f32[8,4,128,128]{3,2,1,0:T(8,128)} async-done(((f32[1,4,128,128]{3,2,1,0:T(8,128)}), f32[8,4,128,128]{3,2,1,0:T(8,128)}) %all-gather.11.cloned.1.call-update) | async-done | bytes 2097168 | tf_op jit(solution)/shard_map/all_gather | solution.py:30
  165.4 2.4 multiply_add_fusion
  167.8 0.0 all-gather.13.cloned.1.call-update
  167.8 0.2 all-gather.15.cloned.1.call-start
  168.0 7.5 %fusion.18 = bf16[512,768]{1,0:T(8,128)(2,1)S(1)} fusion(bf16[768,4096]{1,0:T(8,128)(2,1)} %param.8, bf16[4096,1540]{1,0:T(8,128)(2,1)} %all-gather.9.cloned.1.call-done), kind=kOutput, calls=%fused_computation.22 | convolution fusion | flops 3221618688 | bytes 11272192 | tf_op jit(solution)/shard_map/dot_general | solution.py:49
  175.6 7.7 %all-gather.3 = f32[4,1,4]{2,1,0:T(1,128)S(1)} all-gather(f32[1,1,4]{2,1,0:T(1,128)S(1)} %get-tuple-element.10), channel_id=1, replica_groups=mesh['seq_0'=4,'seq_1'=8,'seq_2'=2,'tp'=4] {'seq_0'}, dimensions={0}, use_global_device_ids=true | all-gather | bytes 80 | tf_op jit(solution)/shard_map/all_gather | solution.py:30
  183.2 0.4 copy.28
  183.7 6.7 %fusion = f32[4,128,768]{2,1,0:T(8,128)} fusion(bf16[768,4,128]{0,2,1:T(8,128)(2,1)} %bitcast.245, f32[4,768]{1,0:T(4,128)S(1)} %get-tuple-element.9, pred[768,768]{1,0:T(8,128)(4,1)S(1)} %iota_compare_fusion, bf16[768,4,128]{0,2,1:T(8,128)(2,1)S(1)} %bitcast.240, bf16[768,4,128]{0,2,1:T(8,128)(2,1)} %bitcast.247), kind=kOutput, calls=%fused_computation.1 | convolution fusion | flops 1219756032 | bytes 4534272 | tf_op jit(solution)/shard_map/hts,shv->thv/dot_general | solution.py:92
  190.3 5.0 %all-gather.13.cloned.1.call-done = f32[4,4,128,128]{3,2,1,0:T(8,128)} async-done(((f32[1,4,128,128]{3,2,1,0:T(8,128)}), f32[4,4,128,128]{3,2,1,0:T(8,128)}) %all-gather.13.cloned.1.call-update) | async-done | bytes 1048592 | tf_op jit(solution)/shard_map/all_gather | solution.py:30
  195.3 0.0 copy-start
  195.3 3.5 %fusion.11 = (f32[768,4]{0,1:T(4,128)S(1)}, f32[4,128,768]{2,1,0:T(8,128)S(1)}) fusion(f32[4,128,768]{2,1,0:T(8,128)} %fusion, bf16[768,4,128]{2,0,1:T(8,128)(2,1)S(1)} %copy.28, f32[768,4]{0,1:T(4,128)S(1)} %get-tuple-element.8, f32[4,4,128,128]{3,2,1,0:T(8,128)} %all-gather.13.cloned.1.call-done, f32[8,4,128,128]{3,2,1,0:T(8,128)} %all-gather.11.cloned.1.call-done, ...), kind=kOutput, calls=%fused_computation.16 | convolution fusion | flops 105903104 | bytes 7627022 | tf_op jit(solution)/shard_map/fys,ysu->fyu/dot_general | solution.py:78
  198.9 0.1 bitcast_multiply_fusion.1
  199.0 0.0 copy-done
  199.0 1.0 fusion.10
  200.1 0.0 all-gather.15.cloned.1.call-update
  200.1 44.4 %all-gather.15.cloned.1.call-done = bf16[768,2048]{0,1:T(8,128)(2,1)} async-done(((bf16[768,512]{0,1:T(8,128)(2,1)}), bf16[768,2048]{0,1:T(8,128)(2,1)}) %all-gather.15.cloned.1.call-update) | async-done | bytes 3145744 | tf_op jit(solution)/shard_map/all_gather | solution.py:102
  244.5 7.8 %convolution_convert_fusion = bf16[768,1024]{1,0:T(8,128)(2,1)} fusion(bf16[768,2048]{0,1:T(8,128)(2,1)} %all-gather.15.cloned.1.call-done, bf16[2048,1024]{1,0:T(8,128)(2,1)} %param.15), kind=kOutput, calls=%fused_computation.11 | convolution fusion | flops 3222011904 | bytes 8912896 | tf_op jit(solution)/shard_map/dot_general | solution.py:101
  (10 shorter events, 0.1 us)
Async XLA Ops:
  6.5 99.7 %all-gather.9.cloned.1.call-start = ((), (), s32[]{:S(2)}) async-start(), calls=%async_computation | async-start | bytes 13844480 | tf_op jit(solution)/shard_map/all_gather | solution.py:12
  8.9 156.4 %all-gather.11.cloned.1.call-start = ((), (), s32[]{:S(2)}) async-start(), calls=%async_computation.1 | async-start | bytes 2359296 | tf_op jit(solution)/shard_map/all_gather | solution.py:30
  106.2 14.6 %slice-start = ((s8[6291456]{0:T(1024)(128)(4,1)}), s8[2097152]{0:T(1024)(128)(4,1)S(1)}, s32[]{:S(2)}) async-start(s8[6291456]{0:T(1024)(128)(4,1)} %bitcast.237), calls=%async_computation.4 | async-start | bytes 4194304
  113.1 7.7 %slice-start.1 = ((s8[6291456]{0:T(1024)(128)(4,1)}), s8[4194304]{0:T(1024)(128)(4,1)S(1)}, s32[]{:S(2)}) async-start(s8[6291456]{0:T(1024)(128)(4,1)} %bitcast.237), calls=%async_computation.5 | async-start | bytes 8388608
  120.8 6.0 %copy-start.1 = (bf16[512,768]{1,0:T(8,128)(2,1)}, bf16[512,768]{1,0:T(8,128)(2,1)S(1)}, u32[]{:S(2)}) copy-start(bf16[512,768]{1,0:T(8,128)(2,1)S(1)} %fusion.15) | copy-start | bytes 2359300
  126.7 4.4 %copy-start.2 = (bf16[512,768]{1,0:T(8,128)(2,1)}, bf16[512,768]{1,0:T(8,128)(2,1)S(1)}, u32[]{:S(2)}) copy-start(bf16[512,768]{1,0:T(8,128)(2,1)S(1)} %fusion.12) | copy-start | bytes 2359300
  131.9 63.4 %all-gather.13.cloned.1.call-start = ((), (), s32[]{:S(2)}) async-start(), calls=%async_computation.2 | async-start | bytes 1310720 | tf_op jit(solution)/shard_map/all_gather | solution.py:30
  167.8 76.7 %all-gather.15.cloned.1.call-start = ((), (), s32[]{:S(2)}) async-start(), calls=%async_computation.3 | async-start | bytes 3932160 | tf_op jit(solution)/shard_map/all_gather | solution.py:102
  195.3 3.7 %copy-start = (f32[512]{0:T(512)S(1)}, f32[512]{0:T(512)}, u32[]{:S(2)}) copy-start(f32[512]{0:T(512)} %param.14) | copy-start | bytes 6148
Sparse Core Ops, SparseCore 0:
  10.1 96.0 all-gather.8
  132.1 33.2 all-gather.10
  167.9 27.3 all-gather.12
  200.2 44.2 all-gather.14
where the time goes:
time: 259 us
  waiting for transfers between devices  168 us (65%)
  matrix products  44.5 us (17%)
  blocking collectives  22.8 us (9%)
  between operations  13.3 us (5%)
  other arithmetic  8.38 us (3%)
    all_gather x1, waiting for transfers between devices, side_by_side(): lax.all_gather(both, axis, axis=dim, tiled=True)  96.5 us
    all_gather x1, waiting for transfers between devices, on_device(): lax.all_gather(normed, 'tp', axis=1, tiled=True)  44.4 us
    all_gather x2, waiting for transfers between devices, carried_in(): pieces = jax.tree.map(lambda part: lax.all_gather(part, axis), so_far)  27 us
    dot_general x4, matrix products, contract(): return jnp.dot(tokens, piece, preferred_element_type=jnp.float32)  26.1 us
    all_gather x4, blocking collectives, carried_in(): pieces = jax.tree.map(lambda part: lax.all_gather(part, axis), so_far)  22.8 us
    dot_general x1, matrix products, on_device(): jnp.dot(lax.all_gather(normed, 'tp', axis=1, tiled=True), out_weight, pre...  7.75 us
    dot_general x1, matrix products, on_device(): jnp.einsum('hts,shv->thv', attn, value_per_head, preferred_element_type=j...  6.66 us
  transfers between devices with their start and end apart: 4, of which 4 were waited for; matrix products, arithmetic and copies ran while one was open for 6% of the time, Pallas kernels for 0%

commit v1 on v0

--- a/solution.py
+++ b/solution.py
@@ -5,6 +5,27 @@
 from jax.sharding import PartitionSpec as P
 
 SEQ = ("seq_0", "seq_1", "seq_2")
+
+
+def ring_gather(shard, axis, dim):
+    devices, here, rows = (lax.axis_size(axis), lax.axis_index(axis), shard.shape[dim])
+    ahead = [(i, (i + 1) % devices) for i in range(devices)]
+    left = [(i, (i - 1) % devices) for i in range(devices)]
+    filled = jnp.zeros((*shard.shape[:dim], devices * rows, *shard.shape[dim + 1 :]), shard.dtype)
+    filled = lax.dynamic_update_slice_in_dim(filled, shard, here * rows, axis=dim)
+    from_left = from_right = shard
+    middle = devices // 2
+    for turn in range(1, middle + 1):
+        from_left = lax.ppermute(from_left, axis, ahead)
+        filled = lax.dynamic_update_slice_in_dim(
+            filled, from_left, (here - turn) % devices * rows, axis=dim
+        )
+        if turn < devices - middle:
+            from_right = lax.ppermute(from_right, axis, left)
+            filled = lax.dynamic_update_slice_in_dim(
+                filled, from_right, (here + turn) % devices * rows, axis=dim
+            )
+    return filled
 
 
 def side_by_side(arrays, axis, dim, along):
@@ -98,11 +119,7 @@
         None, :
     ]
     normed = normed.astype(jnp.bfloat16)
-    mixed = jnp.dot(
-        lax.all_gather(normed, "tp", axis=1, tiled=True),
-        out_weight,
-        preferred_element_type=jnp.float32,
-    )
+    mixed = jnp.dot(ring_gather(normed, "tp", 1), out_weight, preferred_element_type=jnp.float32)
     return mixed.astype(jnp.bfloat16)
 
 

time: 259 us -> 251 us (0.969); the launches traced: 259 us -> 248 us
  waiting for transfers between devices: 168 us -> 153 us
  local copies, waits for them, and re-layouts: 1.55 us -> 5.96 us
  matrix products: 44.5 us -> 41.2 us
    all_gather x1 -> x0, waiting for transfers between devices: 44.4 us -> none  [on_device(): lax.all_gather(normed, 'tp', axis=1, tiled=True)]
    ppermute x0 -> x3, waiting for transfers between devices: none -> 29.5 us  [the longest x2 29.5 us: ring_gather(): from_left = lax.ppermute(from_left, axis, ahead)]
    dynamic_update_slice x0 -> x3, local copies, waits for them, and re-layouts: none -> 3.86 us  [the longest x2 2.53 us: ring_gather(): lax.dynamic_update_slice_in_dim(filled, from_left, (here - turn) % device...]
    dot_general x1, matrix products: 7.75 us -> 4.56 us  [on_device(): jnp.dot(ring_gather(normed, 'tp', 1), out_weight, preferred_element_type=...]
    ppermute x0 -> x3, starting transfers between devices: none -> 2.68 us  [the longest x1 1.49 us: ring_gather(): from_right = lax.ppermute(from_right, axis, left)]
  transfers between devices with their start and end apart: 4 -> 6, of which waited for: 4 -> 5; matrix products, arithmetic and copies ran while one was open for 6% -> 7% of each run, Pallas kernels for 0% -> 0%
where the time goes in v1:
time: 251 us; the launch traced here: 248 us
  waiting for transfers between devices  153 us (61%)
  matrix products  41.2 us (16%)
  blocking collectives  23 us (9%)
  between operations  13.3 us (5%)
  other arithmetic  8.38 us (3%)
  local copies, waits for them, and re-layouts  5.96 us (2%)
  starting transfers between devices  2.76 us (1%)
    all_gather x1, waiting for transfers between devices, side_by_side(): lax.all_gather(both, axis, axis=dim, tiled=True)  96.5 us
    ppermute x2, waiting for transfers between devices, ring_gather(): from_left = lax.ppermute(from_left, axis, ahead)  29.5 us
    all_gather x2, waiting for transfers between devices, carried_in(): pieces = jax.tree.map(lambda part: lax.all_gather(part, axis), so_far)  27 us
    dot_general x4, matrix products, contract(): return jnp.dot(tokens, piece, preferred_element_type=jnp.float32)  26.1 us
    all_gather x4, blocking collectives, carried_in(): pieces = jax.tree.map(lambda part: lax.all_gather(part, axis), so_far)  23 us
    dot_general x1, matrix products, on_device(): jnp.einsum('hts,shv->thv', attn, value_per_head, preferred_element_type=j...  6.64 us
  transfers between devices with their start and end apart: 6, of which 5 were waited for; matrix products, arithmetic and copies ran while one was open for 7% of the time, Pallas kernels for 0%

profile of v1, /device:TPU:1, one launch (start us, length us, event | category | flops | bytes accessed | tf_op | source)
XLA Modules:
  0.0 247.8 jit_solution(10483470566070652166)
XLA Ops:
  6.5 0.0 all-gather.8.cloned.1.call-start
  6.5 0.8 copy.26
  7.3 1.6 pad_maximum_fusion
  8.9 0.0 all-gather.8.cloned.1.call-update
  8.9 0.0 all-gather.10.cloned.1.call-start
  9.0 0.7 neg.9
  9.7 96.5 %all-gather.8.cloned.1.call-done = bf16[4096,1540]{1,0:T(8,128)(2,1)} async-done(((bf16[64,1540]{1,0:T(8,128)(2,1)}), bf16[4096,1540]{1,0:T(8,128)(2,1)}) %all-gather.8.cloned.1.call-update) | async-done | bytes 12615696 | tf_op jit(solution)/shard_map/all_gather | solution.py:33
  106.2 0.0 slice-start
  106.2 5.0 %fusion.70 = f32[4,768]{1,0:T(4,128)S(1)} fusion(bf16[768,4096]{1,0:T(8,128)(2,1)} %param.8, bf16[4096,1540]{1,0:T(8,128)(2,1)} %all-gather.8.cloned.1.call-done, f32[4]{0:T(128)S(1)} %neg.9), kind=kOutput, calls=%fused_computation.90 | convolution fusion | flops 25187328 | bytes 7352336 | tf_op jit(solution)/shard_map/dot_general | solution.py:70
  111.2 1.1 reduce-window.6
  112.4 0.2 slice_reduce_fusion
  112.5 0.2 reduce-window.9
  112.7 0.1 add_bitcast_fusion
  112.8 0.2 slice_reduce_fusion.1
  113.0 0.1 subtract_exponential_fusion
  113.1 1.8 all-gather.1
  114.9 0.0 slice-start.1
  114.9 7.7 %fusion.15 = bf16[512,768]{1,0:T(8,128)(2,1)S(1)} fusion(bf16[768,4096]{1,0:T(8,128)(2,1)} %param.8, bf16[4096,1540]{1,0:T(8,128)(2,1)} %all-gather.8.cloned.1.call-done), kind=kOutput, calls=%fused_computation.21 | convolution fusion | flops 3221618688 | bytes 11272192 | tf_op jit(solution)/shard_map/dot_general | solution.py:70
  122.6 0.0 slice-done
  122.6 0.0 slice-done.1
  122.6 0.0 copy-start.2
  122.6 5.9 %fusion.12 = bf16[512,768]{1,0:T(8,128)(2,1)S(1)} fusion(bf16[768,4096]{1,0:T(8,128)(2,1)S(1)} %bitcast.238, bf16[4096,1540]{1,0:T(8,128)(2,1)} %all-gather.8.cloned.1.call-done), kind=kOutput, calls=%fused_computation.20 | convolution fusion | flops 3221618688 | bytes 11272192 | tf_op jit(solution)/shard_map/dot_general | solution.py:70
  128.5 0.0 copy-start.3
  128.6 0.0 copy-done.2
  128.6 0.4 fusion.23
  128.9 2.2 all-gather
  131.1 0.0 copy-done.3
  131.1 0.8 bitcast_add_fusion.8
  131.9 0.0 all-gather.10.cloned.1.call-update
  131.9 0.0 all-gather.12.cloned.1.call-start
  132.0 0.2 iota_compare_fusion
  132.2 11.3 %all-gather.2 = f32[8,1,4]{2,1,0:T(1,128)S(1)} all-gather(f32[1,1,4]{2,1,0:T(1,128)S(1)} %get-tuple-element.23), channel_id=1, replica_groups=mesh['seq_0'=4,'seq_1'=8,'seq_2'=2,'tp'=4] {'seq_1'}, dimensions={0}, use_global_device_ids=true | all-gather | bytes 144 | tf_op jit(solution)/shard_map/all_gather | solution.py:51
  143.6 21.8 %all-gather.10.cloned.1.call-done = f32[8,4,128,128]{3,2,1,0:T(8,128)} async-done(((f32[1,4,128,128]{3,2,1,0:T(8,128)}), f32[8,4,128,128]{3,2,1,0:T(8,128)}) %all-gather.10.cloned.1.call-update) | async-done | bytes 2097168 | tf_op jit(solution)/shard_map/all_gather | solution.py:51
  165.4 2.4 multiply_add_fusion
  167.8 0.0 all-gather.12.cloned.1.call-update
  167.8 7.5 %fusion.18 = bf16[512,768]{1,0:T(8,128)(2,1)S(1)} fusion(bf16[768,4096]{1,0:T(8,128)(2,1)} %param.8, bf16[4096,1540]{1,0:T(8,128)(2,1)} %all-gather.8.cloned.1.call-done), kind=kOutput, calls=%fused_computation.22 | convolution fusion | flops 3221618688 | bytes 11272192 | tf_op jit(solution)/shard_map/dot_general | solution.py:70
  175.4 7.7 %all-gather.3 = f32[4,1,4]{2,1,0:T(1,128)S(1)} all-gather(f32[1,1,4]{2,1,0:T(1,128)S(1)} %get-tuple-element.10), channel_id=1, replica_groups=mesh['seq_0'=4,'seq_1'=8,'seq_2'=2,'tp'=4] {'seq_0'}, dimensions={0}, use_global_device_ids=true | all-gather | bytes 80 | tf_op jit(solution)/shard_map/all_gather | solution.py:51
  183.1 0.4 copy.28
  183.5 6.6 %fusion = f32[4,128,768]{2,1,0:T(8,128)} fusion(bf16[768,4,128]{0,2,1:T(8,128)(2,1)} %bitcast.245, f32[4,768]{1,0:T(4,128)S(1)} %get-tuple-element.9, pred[768,768]{1,0:T(8,128)(4,1)S(1)} %iota_compare_fusion, bf16[768,4,128]{0,2,1:T(8,128)(2,1)S(1)} %bitcast.240, bf16[768,4,128]{0,2,1:T(8,128)(2,1)} %bitcast.247), kind=kOutput, calls=%fused_computation.1 | convolution fusion | flops 1219756032 | bytes 4534272 | tf_op jit(solution)/shard_map/hts,shv->thv/dot_general | solution.py:113
  190.1 5.2 %all-gather.12.cloned.1.call-done = f32[4,4,128,128]{3,2,1,0:T(8,128)} async-done(((f32[1,4,128,128]{3,2,1,0:T(8,128)}), f32[4,4,128,128]{3,2,1,0:T(8,128)}) %all-gather.12.cloned.1.call-update) | async-done | bytes 1048592 | tf_op jit(solution)/shard_map/all_gather | solution.py:51
  195.3 3.5 %fusion.11 = (f32[768,4]{0,1:T(4,128)S(1)}, f32[4,128,768]{2,1,0:T(8,128)S(1)}) fusion(f32[4,128,768]{2,1,0:T(8,128)} %fusion, bf16[768,4,128]{2,0,1:T(8,128)(2,1)S(1)} %copy.28, f32[768,4]{0,1:T(4,128)S(1)} %get-tuple-element.8, f32[4,4,128,128]{3,2,1,0:T(8,128)} %all-gather.12.cloned.1.call-done, f32[8,4,128,128]{3,2,1,0:T(8,128)} %all-gather.10.cloned.1.call-done, ...), kind=kOutput, calls=%fused_computation.16 | convolution fusion | flops 105903104 | bytes 7627022 | tf_op jit(solution)/shard_map/fys,ysu->fyu/dot_general | solution.py:99
  198.9 0.0 copy-start
  198.9 0.1 bitcast_multiply_fusion.1
  199.0 0.2 broadcast_in_dim.18
  199.2 0.3 copy-done
  199.5 1.0 constant_dynamic-update-slice_fusion.3
  200.6 1.2 collective-permute-start
  201.8 1.5 collective-permute-start.1
  203.3 15.2 %collective-permute-done = bf16[768,512]{0,1:T(8,128)(2,1)} collective-permute-done((bf16[768,512]{0,1:T(8,128)(2,1)}, bf16[768,512]{0,1:T(8,128)(2,1)}, u32[]{:S(2)}, u32[]{:S(2)}) %collective-permute-start) | collective-permute-done | bytes 786464 | tf_op jit(solution)/shard_map/ppermute | solution.py:19
  218.5 0.0 collective-permute-start.2
  218.5 0.0 copy-start.1
  218.5 1.3 constant_dynamic-update-slice_fusion.2
  219.8 0.0 collective-permute-done.1
  219.8 1.3 constant_dynamic-update-slice_fusion.1
  221.2 14.3 %collective-permute-done.2 = bf16[768,512]{0,1:T(8,128)(2,1)} collective-permute-done((bf16[768,512]{0,1:T(8,128)(2,1)}, bf16[768,512]{0,1:T(8,128)(2,1)}, u32[]{:S(2)}, u32[]{:S(2)}) %collective-permute-start.2) | collective-permute-done | bytes 786464 | tf_op jit(solution)/shard_map/ppermute | solution.py:19
  235.5 1.2 constant_dynamic-update-slice_fusion
  236.7 0.0 copy-done.1
  236.7 4.6 %convolution_convert_fusion = bf16[768,1024]{1,0:T(8,128)(2,1)} fusion(bf16[768,2048]{0,1:T(8,128)(2,1)S(1)} %constant_dynamic-update-slice_fusion, bf16[2048,1024]{1,0:T(8,128)(2,1)S(1)} %copy-done.1), kind=kOutput, calls=%fused_computation.11 | convolution fusion | flops 3222011904 | bytes 8912896 | tf_op jit(solution)/shard_map/dot_general | solution.py:122
  (10 shorter events, 0.1 us)
Async XLA Ops:
  6.5 99.7 %all-gather.8.cloned.1.call-start = ((), (), s32[]{:S(2)}) async-start(), calls=%async_computation | async-start | bytes 13844480 | tf_op jit(solution)/shard_map/all_gather | solution.py:33
  8.9 156.4 %all-gather.10.cloned.1.call-start = ((), (), s32[]{:S(2)}) async-start(), calls=%async_computation.1 | async-start | bytes 2359296 | tf_op jit(solution)/shard_map/all_gather | solution.py:51
  106.2 16.4 %slice-start = ((s8[6291456]{0:T(1024)(128)(4,1)}), s8[2097152]{0:T(1024)(128)(4,1)S(1)}, s32[]{:S(2)}) async-start(s8[6291456]{0:T(1024)(128)(4,1)} %bitcast.237), calls=%async_computation.3 | async-start | bytes 4194304
  114.9 7.7 %slice-start.1 = ((s8[6291456]{0:T(1024)(128)(4,1)}), s8[4194304]{0:T(1024)(128)(4,1)S(1)}, s32[]{:S(2)}) async-start(s8[6291456]{0:T(1024)(128)(4,1)} %bitcast.237), calls=%async_computation.4 | async-start | bytes 8388608
  122.6 6.0 %copy-start.2 = (bf16[512,768]{1,0:T(8,128)(2,1)}, bf16[512,768]{1,0:T(8,128)(2,1)S(1)}, u32[]{:S(2)}) copy-start(bf16[512,768]{1,0:T(8,128)(2,1)S(1)} %fusion.15) | copy-start | bytes 2359300
  128.5 2.6 %copy-start.3 = (bf16[512,768]{1,0:T(8,128)(2,1)}, bf16[512,768]{1,0:T(8,128)(2,1)S(1)}, u32[]{:S(2)}) copy-start(bf16[512,768]{1,0:T(8,128)(2,1)S(1)} %fusion.12) | copy-start | bytes 2359300
  131.9 63.4 %all-gather.12.cloned.1.call-start = ((), (), s32[]{:S(2)}) async-start(), calls=%async_computation.2 | async-start | bytes 1310720 | tf_op jit(solution)/shard_map/all_gather | solution.py:51
  198.9 0.7 copy-start
  200.6 17.9 %collective-permute-start = (bf16[768,512]{0,1:T(8,128)(2,1)}, bf16[768,512]{0,1:T(8,128)(2,1)}, u32[]{:S(2)}, u32[]{:S(2)}) collective-permute-start(bf16[768,512]{0,1:T(8,128)(2,1)} %get-tuple-element.29), channel_id=1, source_target_pairs={{0,1},{1,2},{2,3},{3,0},{4,5},{5,6},{6,7},{7,4},{8,9},{9,10},{10,1... | collective-permute-start | bytes 2359304 | tf_op jit(solution)/shard_map/ppermute | solution.py:19
  201.8 18.0 %collective-permute-start.1 = (bf16[768,512]{0,1:T(8,128)(2,1)}, bf16[768,512]{0,1:T(8,128)(2,1)}, u32[]{:S(2)}, u32[]{:S(2)}) collective-permute-start(bf16[768,512]{0,1:T(8,128)(2,1)} %get-tuple-element.29), channel_id=1, source_target_pairs={{0,3},{1,0},{2,1},{3,2},{4,7},{5,4},{6,5},{7,6},{8,11},{9,8},{10,9... | collective-permute-start | bytes 2359304 | tf_op jit(solution)/shard_map/ppermute | solution.py:24
  218.5 17.0 %collective-permute-start.2 = (bf16[768,512]{0,1:T(8,128)(2,1)}, bf16[768,512]{0,1:T(8,128)(2,1)}, u32[]{:S(2)}, u32[]{:S(2)}) collective-permute-start(bf16[768,512]{0,1:T(8,128)(2,1)} %collective-permute-done), channel_id=1, source_target_pairs={{0,1},{1,2},{2,3},{3,0},{4,5},{5,6},{6,7},{7,4},{8,9},{9,10},{10,1... | collective-permute-start | bytes 2359304 | tf_op jit(solution)/shard_map/ppermute | solution.py:19
  218.5 18.2 %copy-start.1 = (bf16[2048,1024]{1,0:T(8,128)(2,1)S(1)}, bf16[2048,1024]{1,0:T(8,128)(2,1)}, u32[]{:S(2)}) copy-start(bf16[2048,1024]{1,0:T(8,128)(2,1)} %param.15) | copy-start | bytes 12582916
Sparse Core Ops, SparseCore 0:
  10.1 96.0 all-gather.7
  132.1 33.2 all-gather.9
  167.9 27.3 all-gather.11
